TPU v7x, 32 devices: a whole 2x2x4 slice. The times are simulated.
32 devices in a mesh: img: 2 (over x), neu: 16 (over z, y, core).
Axes of the slice: x: 2, y: 2, z: 4, core: 2. Of those that a mesh axis runs over, the one named last changes fastest.
Arguments:
- image_values: bfloat16 [4096, 1024], P('neu', 'img'), may hold values from 0.25 to 16
- image_mask: int32 [4096, 1024], P('neu', 'img'), may hold values 0 or 1
- weights: bfloat16 [3, 4096, 4, 8], P(None, 'neu'), may hold values from -0.25 to 0.34960938
- block_index: int32 [3, 128, 4], P(None, 'neu'), may hold values from 0 to 511, as said below
Outputs:
- activations: bfloat16 [4096, 1024], P('neu', 'img')
- row_sums: float32 [1024], P(('img', 'neu'))
Inputs may be any that keep to these rules, and one draw needn't show every extreme that they name: Split the 512 input blocks into 16 runs of consecutive blocks, and the 128 output blocks likewise; if output block b lies in run s, block_index[l, b, k] lies in run (s + k * 4 + l) mod 16.
All inputs are finite; a program needn't handle non-finite values. No bound on the sum of `image_mask` on one device may be relied on, other than what follows from the above.
Results may differ from a plain program's by a relative error of at most 0.0035.
Values may be sent and summed in bfloat16 or wider, within the bound.
A program may use at most 64 MiB of HBM per device.

v0:
```python
import jax
import jax.numpy as jnp
from jax import lax
from jax.sharding import PartitionSpec as P

KB = 4
IB = 8
OB = 32


bias_value = 0.35
ceiling = 32.0


def from_behind(block, axis, distance):
    devices = range(lax.axis_size(axis))
    route = [((i - distance) % len(devices), i) for i in devices]
    return lax.ppermute(block, axis, route)


def contract(layer_weights, picked, blocks_count):
    weights_view = layer_weights.reshape(blocks_count, OB, KB * IB)
    picked_view = picked.reshape(blocks_count, KB * IB, -1)
    summed = jnp.einsum(
        "dom,dmr->dor", weights_view, picked_view, preferred_element_type=jnp.float32
    )
    clamped = jnp.minimum(jnp.maximum(summed - bias_value, 0.0), ceiling)
    return clamped.astype(jnp.bfloat16).reshape(blocks_count * OB, -1)


def on_device(image_values, image_mask, weights, block_index):
    activity = image_values * image_mask.astype(jnp.bfloat16)
    layer_count = weights.shape[0]
    blocks_count = block_index.shape[1]
    columns = activity.shape[1]
    shard_rows = activity.shape[0]
    run_blocks = shard_rows // IB
    devices = lax.axis_size("neu")
    offsets = jnp.arange(IB, dtype=jnp.int32)
    for layer_number in range(layer_count):
        layer_blocks = block_index[layer_number]
        slot_parts = []
        for slot in range(KB):
            distance = (slot * (devices // KB) + layer_number) % devices
            arrived = from_behind(activity, "neu", (devices - distance) % devices)
            local_rows = (
                (layer_blocks[:, slot] % run_blocks)[:, None] * IB + offsets[None, :]
            ).reshape(-1)
            slot_parts.append(
                jnp.take(arrived, local_rows, axis=0).reshape(blocks_count, IB, columns)
            )
        picked = jnp.stack(slot_parts, axis=1).reshape(blocks_count * KB * IB, columns)
        activity = contract(weights[layer_number], picked, blocks_count)
    partial_sums = jnp.sum(activity, axis=0, dtype=jnp.float32)
    totals = lax.psum_scatter(partial_sums, "neu", scatter_dimension=0, tiled=True)
    return (activity, totals)


def solution(mesh):
    in_specs = (P("neu", "img"), P("neu", "img"), P(None, "neu", None, None), P(None, "neu", None))
    out_specs = (P("neu", "img"), P(("img", "neu")))
    return jax.shard_map(
        on_device, mesh=mesh, in_specs=in_specs, out_specs=out_specs, check_vma=False
    )
```

profile of v0, /device:TPU:0, one launch (start us, length us, event | category | flops | bytes accessed | tf_op | source)
XLA Modules:
  0.0 120.0 jit_solution(8872691840605774945)
XLA Ops:
  0.6 1.2 convert_multiply_fusion
  1.8 5.1 %collective-permute-start.1 = (bf16[256,512]{1,0:T(8,128)(2,1)S(1)}, bf16[256,512]{1,0:T(8,128)(2,1)S(1)}, u32[]{:S(2)}, u32[]{:S(2)}) collective-permute-start(bf16[256,512]{1,0:T(8,128)(2,1)S(1)} %convert_multiply_fusion), channel_id=1, source_target_pairs={{4,0},{5,1},{6,2},{7,3},{8,4},{9,5},{10,6},{11,7},{12,8},{13,9},{1... | collective-permute-start | bytes 786440 | tf_op jit(solution)/shard_map/ppermute | solution.py:18
  7.0 1.0 collective-permute-start.3
  10.3 3.4 %collective-permute-done.1 = bf16[256,512]{1,0:T(8,128)(2,1)S(1)} collective-permute-done((bf16[256,512]{1,0:T(8,128)(2,1)S(1)}, bf16[256,512]{1,0:T(8,128)(2,1)S(1)}, u32[]{:S(2)}, u32[]{:S(2)}) %collective-permute-start.1) | collective-permute-done | bytes 262176 | tf_op jit(solution)/shard_map/ppermute | solution.py:18
  13.7 0.7 gather_fusion.1
  14.5 0.7 gather_fusion
  15.3 14.0 %collective-permute-done.2 = bf16[256,512]{1,0:T(8,128)(2,1)S(1)} collective-permute-done((bf16[256,512]{1,0:T(8,128)(2,1)S(1)}, bf16[256,512]{1,0:T(8,128)(2,1)S(1)}, u32[]{:S(2)}, u32[]{:S(2)}) %collective-permute-start.2) | collective-permute-done | bytes 262176 | tf_op jit(solution)/shard_map/ppermute | solution.py:18
  29.2 0.7 gather_fusion.2
  30.0 0.7 gather_fusion.3
  30.8 0.3 fusion.3
  31.3 3.5 %collective-permute-start.5 = (bf16[256,512]{1,0:T(8,128)(2,1)S(1)}, bf16[256,512]{1,0:T(8,128)(2,1)S(1)}, u32[]{:S(2)}, u32[]{:S(2)}) collective-permute-start(bf16[256,512]{1,0:T(8,128)(2,1)S(1)} %bitcast.117), channel_id=1, source_target_pairs={{5,0},{6,1},{7,2},{8,3},{9,4},{10,5},{11,6},{12,7},{13,8},{14,9},{... | collective-permute-start | bytes 786440 | tf_op jit(solution)/shard_map/ppermute | solution.py:18
  34.9 0.7 collective-permute-start.4
  35.7 15.8 %collective-permute-done.6 = bf16[256,512]{1,0:T(8,128)(2,1)S(1)} collective-permute-done((bf16[256,512]{1,0:T(8,128)(2,1)S(1)}, bf16[256,512]{1,0:T(8,128)(2,1)S(1)}, u32[]{:S(2)}, u32[]{:S(2)}) %collective-permute-start.6) | collective-permute-done | bytes 262176 | tf_op jit(solution)/shard_map/ppermute | solution.py:18
  51.5 0.7 gather_fusion.6
  52.3 0.7 gather_fusion.5
  53.1 0.7 gather_fusion.4
  53.9 0.7 gather_fusion.7
  54.6 0.3 fusion.4
  54.9 6.0 %collective-permute-start.10 = (bf16[256,512]{1,0:T(8,128)(2,1)S(1)}, bf16[256,512]{1,0:T(8,128)(2,1)S(1)}, u32[]{:S(2)}, u32[]{:S(2)}) collective-permute-start(bf16[256,512]{1,0:T(8,128)(2,1)S(1)} %bitcast.112), channel_id=1, source_target_pairs={{10,0},{11,1},{12,2},{13,3},{14,4},{15,5},{0,6},{1,7},{2,8},{3,9},... | collective-permute-start | bytes 786440 | tf_op jit(solution)/shard_map/ppermute | solution.py:18
  61.1 0.6 copy-done.2
  61.8 0.6 dynamic-slice
  63.0 2.8 %collective-permute-start.8 = (bf16[256,512]{1,0:T(8,128)(2,1)S(1)}, bf16[256,512]{1,0:T(8,128)(2,1)S(1)}, u32[]{:S(2)}, u32[]{:S(2)}) collective-permute-start(bf16[256,512]{1,0:T(8,128)(2,1)S(1)} %bitcast.114), channel_id=1, source_target_pairs={{2,0},{3,1},{4,2},{5,3},{6,4},{7,5},{8,6},{9,7},{10,8},{11,9},{12,... | collective-permute-start | bytes 786440 | tf_op jit(solution)/shard_map/ppermute | solution.py:18
  65.8 6.9 %collective-permute-done.10 = bf16[256,512]{1,0:T(8,128)(2,1)S(1)} collective-permute-done((bf16[256,512]{1,0:T(8,128)(2,1)S(1)}, bf16[256,512]{1,0:T(8,128)(2,1)S(1)}, u32[]{:S(2)}, u32[]{:S(2)}) %collective-permute-start.10) | collective-permute-done | bytes 262176 | tf_op jit(solution)/shard_map/ppermute | solution.py:18
  72.6 0.7 gather_fusion.10
  73.4 2.8 %collective-permute-done.9 = bf16[256,512]{1,0:T(8,128)(2,1)S(1)} collective-permute-done((bf16[256,512]{1,0:T(8,128)(2,1)S(1)}, bf16[256,512]{1,0:T(8,128)(2,1)S(1)}, u32[]{:S(2)}, u32[]{:S(2)}) %collective-permute-start.9) | collective-permute-done | bytes 262176 | tf_op jit(solution)/shard_map/ppermute | solution.py:18
  76.3 0.7 gather_fusion.9
  77.1 6.3 %collective-permute-done.8 = bf16[256,512]{1,0:T(8,128)(2,1)S(1)} collective-permute-done((bf16[256,512]{1,0:T(8,128)(2,1)S(1)}, bf16[256,512]{1,0:T(8,128)(2,1)S(1)}, u32[]{:S(2)}, u32[]{:S(2)}) %collective-permute-start.8) | collective-permute-done | bytes 262176 | tf_op jit(solution)/shard_map/ppermute | solution.py:18
  83.4 0.7 gather_fusion.8
  84.2 0.7 gather_fusion.11
  84.9 1.0 convert_reduce_fusion
  85.9 33.5 %all-reduce = f32[512]{0:T(512)S(1)} all-reduce(f32[512]{0:T(512)S(1)} %get-tuple-element.21), channel_id=2, replica_groups=mesh['img'=2,'neu'=16] {'neu'}, use_global_device_ids=true, to_apply=%region_1.3.clone | all-reduce | flops 512 | bytes 4096
  119.4 0.6 dynamic-slice.1
  (94 shorter events, 3.6 us)
Async XLA Ops:
  0.6 7.4 %copy-start.1 = (s32[3,8,4]{1,2,0:T(4,128)S(1)}, s32[3,8,4]{1,2,0:T(4,128)}, u32[]{:S(2)}) copy-start(s32[3,8,4]{1,2,0:T(4,128)} %param.9) | copy-start | bytes 1156
  1.8 11.9 %collective-permute-start.1 = (bf16[256,512]{1,0:T(8,128)(2,1)S(1)}, bf16[256,512]{1,0:T(8,128)(2,1)S(1)}, u32[]{:S(2)}, u32[]{:S(2)}) collective-permute-start(bf16[256,512]{1,0:T(8,128)(2,1)S(1)} %convert_multiply_fusion), channel_id=1, source_target_pairs={{4,0},{5,1},{6,2},{7,3},{8,4},{9,5},{10,6},{11,7},{12,8},{13,9},{1... | collective-permute-start | bytes 786440 | tf_op jit(solution)/shard_map/ppermute | solution.py:18
  6.9 7.5 %collective-permute-start = (bf16[256,512]{1,0:T(8,128)(2,1)S(1)}, bf16[256,512]{1,0:T(8,128)(2,1)S(1)}, u32[]{:S(2)}, u32[]{:S(2)}) collective-permute-start(bf16[256,512]{1,0:T(8,128)(2,1)S(1)} %convert_multiply_fusion), channel_id=1, source_target_pairs={{0,0},{1,1},{2,2},{3,3},{4,4},{5,5},{6,6},{7,7},{8,8},{9,9},{10,10... | collective-permute-start | bytes 786440 | tf_op jit(solution)/shard_map/ppermute | solution.py:18
  7.0 22.3 %collective-permute-start.2 = (bf16[256,512]{1,0:T(8,128)(2,1)S(1)}, bf16[256,512]{1,0:T(8,128)(2,1)S(1)}, u32[]{:S(2)}, u32[]{:S(2)}) collective-permute-start(bf16[256,512]{1,0:T(8,128)(2,1)S(1)} %convert_multiply_fusion), channel_id=1, source_target_pairs={{8,0},{9,1},{10,2},{11,3},{12,4},{13,5},{14,6},{15,7},{0,8},{1,9},... | collective-permute-start | bytes 786440 | tf_op jit(solution)/shard_map/ppermute | solution.py:18
  7.0 23.0 %collective-permute-start.3 = (bf16[256,512]{1,0:T(8,128)(2,1)S(1)}, bf16[256,512]{1,0:T(8,128)(2,1)S(1)}, u32[]{:S(2)}, u32[]{:S(2)}) collective-permute-start(bf16[256,512]{1,0:T(8,128)(2,1)S(1)} %convert_multiply_fusion), channel_id=1, source_target_pairs={{12,0},{13,1},{14,2},{15,3},{0,4},{1,5},{2,6},{3,7},{4,8},{5,9},{6... | collective-permute-start | bytes 786440 | tf_op jit(solution)/shard_map/ppermute | solution.py:18
  9.3 0.8 copy-start
  31.1 20.4 %collective-permute-start.6 = (bf16[256,512]{1,0:T(8,128)(2,1)S(1)}, bf16[256,512]{1,0:T(8,128)(2,1)S(1)}, u32[]{:S(2)}, u32[]{:S(2)}) collective-permute-start(bf16[256,512]{1,0:T(8,128)(2,1)S(1)} %bitcast.116), channel_id=1, source_target_pairs={{9,0},{10,1},{11,2},{12,3},{13,4},{14,5},{15,6},{0,7},{1,8},{2,9},... | collective-permute-start | bytes 786440 | tf_op jit(solution)/shard_map/ppermute | solution.py:18
  31.3 21.0 %collective-permute-start.5 = (bf16[256,512]{1,0:T(8,128)(2,1)S(1)}, bf16[256,512]{1,0:T(8,128)(2,1)S(1)}, u32[]{:S(2)}, u32[]{:S(2)}) collective-permute-start(bf16[256,512]{1,0:T(8,128)(2,1)S(1)} %bitcast.117), channel_id=1, source_target_pairs={{5,0},{6,1},{7,2},{8,3},{9,4},{10,5},{11,6},{12,7},{13,8},{14,9},{... | collective-permute-start | bytes 786440 | tf_op jit(solution)/shard_map/ppermute | solution.py:18
  34.9 18.1 %collective-permute-start.4 = (bf16[256,512]{1,0:T(8,128)(2,1)S(1)}, bf16[256,512]{1,0:T(8,128)(2,1)S(1)}, u32[]{:S(2)}, u32[]{:S(2)}) collective-permute-start(bf16[256,512]{1,0:T(8,128)(2,1)S(1)} %bitcast.118), channel_id=1, source_target_pairs={{1,0},{2,1},{3,2},{4,3},{5,4},{6,5},{7,6},{8,7},{9,8},{10,9},{11,1... | collective-permute-start | bytes 786440 | tf_op jit(solution)/shard_map/ppermute | solution.py:18
  35.7 18.2 %collective-permute-start.7 = (bf16[256,512]{1,0:T(8,128)(2,1)S(1)}, bf16[256,512]{1,0:T(8,128)(2,1)S(1)}, u32[]{:S(2)}, u32[]{:S(2)}) collective-permute-start(bf16[256,512]{1,0:T(8,128)(2,1)S(1)} %bitcast.119), channel_id=1, source_target_pairs={{13,0},{14,1},{15,2},{0,3},{1,4},{2,5},{3,6},{4,7},{5,8},{6,9},{7,... | collective-permute-start | bytes 786440 | tf_op jit(solution)/shard_map/ppermute | solution.py:18
  54.9 17.7 %collective-permute-start.10 = (bf16[256,512]{1,0:T(8,128)(2,1)S(1)}, bf16[256,512]{1,0:T(8,128)(2,1)S(1)}, u32[]{:S(2)}, u32[]{:S(2)}) collective-permute-start(bf16[256,512]{1,0:T(8,128)(2,1)S(1)} %bitcast.112), channel_id=1, source_target_pairs={{10,0},{11,1},{12,2},{13,3},{14,4},{15,5},{0,6},{1,7},{2,8},{3,9},... | collective-permute-start | bytes 786440 | tf_op jit(solution)/shard_map/ppermute | solution.py:18
  60.9 15.3 %collective-permute-start.9 = (bf16[256,512]{1,0:T(8,128)(2,1)S(1)}, bf16[256,512]{1,0:T(8,128)(2,1)S(1)}, u32[]{:S(2)}, u32[]{:S(2)}) collective-permute-start(bf16[256,512]{1,0:T(8,128)(2,1)S(1)} %bitcast.113), channel_id=1, source_target_pairs={{6,0},{7,1},{8,2},{9,3},{10,4},{11,5},{12,6},{13,7},{14,8},{15,9},... | collective-permute-start | bytes 786440 | tf_op jit(solution)/shard_map/ppermute | solution.py:18
  61.1 0.7 copy-start.2
  63.0 20.3 %collective-permute-start.8 = (bf16[256,512]{1,0:T(8,128)(2,1)S(1)}, bf16[256,512]{1,0:T(8,128)(2,1)S(1)}, u32[]{:S(2)}, u32[]{:S(2)}) collective-permute-start(bf16[256,512]{1,0:T(8,128)(2,1)S(1)} %bitcast.114), channel_id=1, source_target_pairs={{2,0},{3,1},{4,2},{5,3},{6,4},{7,5},{8,6},{9,7},{10,8},{11,9},{12,... | collective-permute-start | bytes 786440 | tf_op jit(solution)/shard_map/ppermute | solution.py:18
  65.8 18.4 %collective-permute-start.11 = (bf16[256,512]{1,0:T(8,128)(2,1)S(1)}, bf16[256,512]{1,0:T(8,128)(2,1)S(1)}, u32[]{:S(2)}, u32[]{:S(2)}) collective-permute-start(bf16[256,512]{1,0:T(8,128)(2,1)S(1)} %bitcast.115), channel_id=1, source_target_pairs={{14,0},{15,1},{0,2},{1,3},{2,4},{3,5},{4,6},{5,7},{6,8},{7,9},{8,1... | collective-permute-start | bytes 786440 | tf_op jit(solution)/shard_map/ppermute | solution.py:18
where the time goes:
time: 120 us
  waiting for transfers between devices  49.2 us (41%)
  blocking collectives  33.5 us (28%)
  starting transfers between devices  19.5 us (16%)
  local copies, waits for them, and re-layouts  11.6 us (10%)
  other arithmetic  3.09 us (3%)
  between operations  1.63 us (1%)
  matrix products  1.53 us (1%)
    ppermute x12, waiting for transfers between devices, from_behind(): return lax.ppermute(block, axis, route)  49.2 us
    unnamed x1, blocking collectives  33.5 us
    ppermute x12, starting transfers between devices, from_behind(): return lax.ppermute(block, axis, route)  19.5 us
    gather x12, local copies, waits for them, and re-layouts, on_device(): jnp.take(arrived, local_rows, axis=0).reshape(blocks_count, IB, columns)  8.41 us
  transfers between devices with their start and end apart: 12, of which 6 were waited for; matrix products, arithmetic and copies ran while one was open for 8% of the time, Pallas kernels for 0%

commit v1 on v0

v1 whole, which is shorter than its diff:
```python
import functools

import jax
import jax.numpy as jnp
from jax import lax
from jax.experimental import pallas as pl
from jax.experimental.pallas import tpu as pltpu
from jax.sharding import PartitionSpec as P

KB = 4
IB = 8
OB = 32

bias_value = 0.35
ceiling = 32.0


def quotient(x, n):
    return x >> (n.bit_length() - 1) if n & (n - 1) == 0 else lax.div(x, jnp.int32(n))


def remainder(x, n):
    return x & (n - 1) if n & (n - 1) == 0 else lax.rem(x, jnp.int32(n))


def kernel(
    geometry, val_hbm, mask_hbm, wt_hbm, idx_hbm, out_ref, rs_ref,
    val, mask, y0, xin, ya, yb, wt, wd, idx_v, idx_s, tiles, part, parts,
    load_sem, in_send, in_recv, w_send, w_recv, i_send, i_recv, s_sem, o_send, o_recv, r_send, r_recv,
):
    classes, layers, rows, blocks, lanes = geometry
    group = KB
    devices = classes * group
    shift = [l * (l + 1) // 2 for l in range(layers)]
    me = lax.axis_index("neu")
    q, c = me // classes, me % classes
    run_blocks = rows // IB

    def device(dq, dc):
        return ((q + dq) % group) * classes + (c + dc) % classes

    def remote(src, dst, send, recv, dq, dc):
        return pltpu.make_async_remote_copy(
            src_ref=src, dst_ref=dst, send_sem=send, recv_sem=recv,
            device_id={"neu": device(dq, dc)}, device_id_type=pl.DeviceIdType.MESH,
        )

    order = [d for d in (2, 1, 3)]

    loads = []
    for n, d in enumerate(order + [0]):
        t = (q + d) % group
        cols = pl.ds(pl.multiple_of(t * lanes, lanes), lanes)
        a = pltpu.make_async_copy(val_hbm.at[:, cols], val.at[d], load_sem.at[0, d])
        b = pltpu.make_async_copy(mask_hbm.at[:, cols], mask.at[d], load_sem.at[1, d])
        a.start()
        b.start()
        loads.append((d, a, b))

    partners = set()
    for dq in range(group):
        for s in shift:
            partners |= {(dq, s % classes), (dq, -s % classes)}
    for dc in range(classes):
        partners.add((0, dc))
    partners.discard((0, 0))
    barrier = pltpu.get_barrier_semaphore()
    for dq, dc in sorted(partners):
        pl.semaphore_signal(
            barrier, inc=1, device_id={"neu": device(dq, dc)},
            device_id_type=pl.DeviceIdType.MESH,
        )
    pl.semaphore_wait(barrier, len(partners))

    waits = []

    def send_weights(l):
        pending = []
        for dq in order + [0]:
            if dq == 0 and shift[l] % classes == 0:
                a = pltpu.make_async_copy(wt_hbm.at[l], wt.at[l, q], w_recv.at[l, 0])
                b = pltpu.make_async_copy(idx_hbm.at[l], idx_v.at[l, q], i_recv.at[l, 0])
                a.start()
                b.start()
                pending += [(a.wait, b.wait)]
                continue
            b = remote(idx_hbm.at[l], idx_v.at[l, q], i_send.at[l, dq], i_recv.at[l, dq], dq, shift[l])
            a = remote(wt_hbm.at[l], wt.at[l, q], w_send.at[l, dq], w_recv.at[l, dq], dq, shift[l])
            b.start()
            a.start()
            waits.extend([a.wait_send, b.wait_send])
            pending += [(a.wait_recv, b.wait_recv)]
        return pending

    pending_w = [None] * layers
    pending_w[0] = send_weights(0)

    inputs = []
    for d, a, b in loads:
        a.wait()
        b.wait()
        masked = (val[d].astype(jnp.float32) * mask[d].astype(jnp.float32))
        if d:
            y0[d] = masked.astype(jnp.bfloat16)
            x = remote(y0.at[d], xin.at[d], in_send.at[d], in_recv.at[d], d, 0)
            x.start()
            waits.append(x.wait_send)
            inputs.append((d, x))
        else:
            ya[pl.ds(q * run_blocks, run_blocks)] = masked.reshape(run_blocks, IB, lanes)
    for l in range(1, layers):
        pending_w[l] = send_weights(l)

    per = min(4, blocks)
    width = per * OB
    m_of = lax.broadcasted_iota(jnp.int32, (width, width), 0) // (KB * IB)
    n_of = lax.broadcasted_iota(jnp.int32, (width, width), 1) // OB

    def prepare(l):
        for a, b in pending_w[l]:
            b()
        c0 = pltpu.make_async_copy(idx_v.at[l], idx_s.at[l], s_sem.at[l])
        c0.start()
        for a, b in pending_w[l]:
            a()
        for t in range(group):
            for g in range(blocks // per):
                w = wt[l, t, :, g * width:(g + 1) * width].astype(jnp.float32)
                wide = jnp.where(m_of == n_of, jnp.concatenate([w] * per, axis=0), 0.0)
                wd[l, t, g] = wide.T.astype(jnp.bfloat16)
        c0.wait()

    def advance(l, src, t):
        out = []
        for g in range(blocks // per):
            pieces = []
            for j in range(g * per, (g + 1) * per):
                for k in range(KB):
                    b = idx_s[l, t, k, j]
                    pieces.append(src[quotient(b, run_blocks * classes) * run_blocks + remainder(b, run_blocks)])
            picked = jnp.concatenate(pieces, axis=0).astype(jnp.bfloat16)
            summed = jnp.dot(wd[l, t, g], picked, preferred_element_type=jnp.float32)
            clamped = jnp.minimum(jnp.maximum(summed - bias_value, 0.0), ceiling)
            out.append(clamped.astype(jnp.bfloat16))
        return out

    prepare(0)
    for d, x in inputs:
        x.wait_recv()
        s = (q + group - d) % group
        ya[pl.ds(s * run_blocks, run_blocks)] = xin[d].astype(jnp.float32).reshape(run_blocks, IB, lanes)

    src, dst = ya, yb
    for l in range(layers - 1):
        for t in range(group):
            for g, y in enumerate(advance(l, src, t)):
                first = t * run_blocks + g * width // IB
                dst[first:first + width // IB] = y.astype(jnp.float32).reshape(width // IB, IB, lanes)
        prepare(l + 1)
        src, dst = dst, src

    total = jnp.zeros((8, lanes), jnp.float32)
    last = layers - 1
    outputs = []
    for d in order + [0]:
        t = (q + d) % group
        for g, y in enumerate(advance(last, src, t)):
            tiles[d, g * width:(g + 1) * width, :] = y
            total = total + jnp.sum(y.astype(jnp.float32).reshape(width // 8, 8, lanes), axis=0)
        x = remote(
            tiles.at[d], out_ref.at[:, pl.ds(pl.multiple_of(q * lanes, lanes), lanes)],
            o_send.at[d], o_recv.at[d], d, -shift[last],
        )
        x.start()
        waits.append(x.wait_send)
        outputs.append(x)

    part[...] = total
    sums = []
    for dc in range(1, classes):
        x = remote(part, parts.at[dc], r_send.at[dc], r_recv.at[dc], 0, dc)
        x.start()
        waits.append(x.wait_send)
        sums.append((dc, x))
    for dc, x in sums:
        x.wait_recv()
        total = total + parts[dc]
    row = jnp.sum(total, axis=0, keepdims=True)
    share = lanes // classes
    mine = jnp.zeros((1, share), jnp.float32)
    for j in range(classes):
        mine = jnp.where(c == j, row[:, j * share:(j + 1) * share], mine)
    rs_ref[...] = mine
    for x in outputs:
        x.wait_recv()
    for w in waits:
        w()


def on_device(classes, image_values, image_mask, weights, block_index):
    layers, rows = weights.shape[:2]
    blocks = block_index.shape[1]
    columns = image_values.shape[1]
    group = KB
    lanes = columns // group
    wt = jnp.transpose(weights, (0, 2, 3, 1)).reshape(layers, KB * IB, rows)
    idx = jnp.transpose(block_index, (0, 2, 1))
    per = min(4, blocks)
    bf16, f32, i32 = jnp.bfloat16, jnp.float32, jnp.int32
    V, S = pltpu.VMEM, pltpu.SMEM
    dma = pltpu.SemaphoreType.DMA
    any_spec = pl.BlockSpec(memory_space=pl.ANY)
    out, sums = pl.pallas_call(
        functools.partial(kernel, (classes, layers, rows, blocks, lanes)),
        out_shape=(
            jax.ShapeDtypeStruct((rows, columns), bf16),
            jax.ShapeDtypeStruct((1, lanes // classes), f32),
        ),
        in_specs=[any_spec] * 4,
        out_specs=(pl.BlockSpec(memory_space=pltpu.VMEM), pl.BlockSpec(memory_space=pltpu.VMEM)),
        scratch_shapes=[
            V((group, rows, lanes), bf16),
            V((group, rows, lanes), i32),
            V((group, rows, lanes), bf16),
            V((group, rows, lanes), bf16),
            V((group * rows // IB, IB, lanes), f32),
            V((group * rows // IB, IB, lanes), f32),
            V((layers, group, KB * IB, rows), bf16),
            V((layers, group, blocks // per, per * OB, per * KB * IB), bf16),
            V((layers, group, KB, blocks), i32),
            S((layers, group, KB, blocks), i32),
            V((group, rows, lanes), bf16),
            V((8, lanes), f32),
            V((classes, 8, lanes), f32),
            dma((2, group)),
            dma((group,)), dma((group,)),
            dma((layers, group)), dma((layers, group)),
            dma((layers, group)), dma((layers, group)),
            dma((layers,)),
            dma((group,)), dma((group,)),
            dma((classes,)), dma((classes,)),
        ],
        compiler_params=pltpu.CompilerParams(collective_id=0, has_side_effects=True),
    )(image_values, image_mask, wt, idx)
    return out, sums.reshape(-1)


def solution(mesh):
    classes = mesh.shape["neu"] // KB
    in_specs = (P("neu", "img"), P("neu", "img"), P(None, "neu", None, None), P(None, "neu", None))
    out_specs = (P("neu", "img"), P(("img", "neu")))
    return jax.shard_map(
        functools.partial(on_device, classes), mesh=mesh, in_specs=in_specs,
        out_specs=out_specs, check_vma=False,
    )
```

time: 120 us -> 30 us (0.25)
  the two profiles are of different devices: /device:TPU:0 before, /device:TPU:1 now
where the time goes in v1:
time: 30 us; the launch traced here: 29.8 us
  Pallas kernels  27 us (90%)
  local copies, waits for them, and re-layouts  2.19 us (7%)
  between operations  0.65 us (2%)
    pallas_call x1, Pallas kernels, on_device(): pl.pallas_call(functools.partial(kernel, (classes, layers, rows, blocks,...  27 us
    unnamed x4, local copies, waits for them, and re-layouts  2.19 us

profile of v1, /device:TPU:1, one launch (start us, length us, event | category | flops | bytes accessed | tf_op | source)
XLA Modules:
  0.0 29.8 jit_solution(17942127159690917913)
XLA Ops:
  0.6 27.0 %shard_map.59 = (bf16[256,512]{1,0:T(8,128)(2,1)}, f32[1,32]{1,0:T(1,128)}) custom-call(bf16[256,512]{1,0:T(8,128)(2,1)} %val_hbm.1, s32[256,512]{1,0:T(8,128)} %mask_hbm.1, bf16[3,32,256]{2,1,0:T(8,128)(2,1)} %bitcast.5, s32[3,4,8]{2,1,0:T(4,128)} %bitcast.6), custom_call_target="tpu_custom_call" | custom-call | tf_op jit(solution)/shard_map/pallas_call | solution.py:213
  27.6 0.0 copy-start
  27.6 1.7 %copy.8 = bf16[256,512]{1,0:T(8,128)(2,1)} copy(bf16[256,512]{1,0:T(8,128)(2,1)} %get-tuple-element.8) | data formatting | bytes 524288
  29.3 0.0 copy-done
  29.3 0.5 %copy.9 = f32[32]{0:T(128)} copy(f32[32]{0:T(128)S(1)} %bitcast.7) | data formatting | bytes 256
Async XLA Ops:
  27.6 1.7 %copy-start = (f32[1,32]{1,0:T(1,128)S(1)}, f32[1,32]{1,0:T(1,128)}, u32[]{:S(2)}) copy-start(f32[1,32]{1,0:T(1,128)} %get-tuple-element.5) | copy-start | bytes 388

commit v2 on v1

--- a/solution.py
+++ b/solution.py
@@ -25,10 +25,10 @@
 
 def kernel(
     geometry, val_hbm, mask_hbm, wt_hbm, idx_hbm, out_ref, rs_ref,
-    val, mask, y0, xin, ya, yb, wt, wd, idx_v, idx_s, tiles, part, parts,
-    load_sem, in_send, in_recv, w_send, w_recv, i_send, i_recv, s_sem, o_send, o_recv, r_send, r_recv,
+    val, mask, w_src, i_src, y0, xin, ya, yb, wt, wd, idx_v, idx_s, tiles, part, parts,
+    load_sem, own_sem, f_send, f_recv, in_send, in_recv, w_send, w_recv, i_send, i_recv, s_sem, o_send, o_recv, r_send, r_recv,
 ):
-    classes, layers, rows, blocks, lanes = geometry
+    classes, pairs, layers, rows, blocks, lanes = geometry
     group = KB
     devices = classes * group
     shift = [l * (l + 1) // 2 for l in range(layers)]
@@ -47,15 +47,22 @@
 
     order = [d for d in (2, 1, 3)]
 
+    own = [
+        pltpu.make_async_copy(wt_hbm, w_src, own_sem.at[0]),
+        pltpu.make_async_copy(idx_hbm, i_src, own_sem.at[1]),
+    ]
     loads = []
-    for n, d in enumerate(order + [0]):
+    for d in order + [0]:
         t = (q + d) % group
         cols = pl.ds(pl.multiple_of(t * lanes, lanes), lanes)
         a = pltpu.make_async_copy(val_hbm.at[:, cols], val.at[d], load_sem.at[0, d])
         b = pltpu.make_async_copy(mask_hbm.at[:, cols], mask.at[d], load_sem.at[1, d])
+        loads.append((d, a, b))
+    for a in own:
+        a.start()
+    for d, a, b in loads:
         a.start()
         b.start()
-        loads.append((d, a, b))
 
     partners = set()
     for dq in range(group):
@@ -65,51 +72,85 @@
         partners.add((0, dc))
     partners.discard((0, 0))
     barrier = pltpu.get_barrier_semaphore()
-    for dq, dc in sorted(partners):
+    for dq, dc in sorted(partners, reverse=True):
         pl.semaphore_signal(
             barrier, inc=1, device_id={"neu": device(dq, dc)},
             device_id_type=pl.DeviceIdType.MESH,
         )
-    pl.semaphore_wait(barrier, len(partners))
-
-    waits = []
-
-    def send_weights(l):
-        pending = []
-        for dq in order + [0]:
-            if dq == 0 and shift[l] % classes == 0:
-                a = pltpu.make_async_copy(wt_hbm.at[l], wt.at[l, q], w_recv.at[l, 0])
-                b = pltpu.make_async_copy(idx_hbm.at[l], idx_v.at[l, q], i_recv.at[l, 0])
-                a.start()
-                b.start()
-                pending += [(a.wait, b.wait)]
-                continue
-            b = remote(idx_hbm.at[l], idx_v.at[l, q], i_send.at[l, dq], i_recv.at[l, dq], dq, shift[l])
-            a = remote(wt_hbm.at[l], wt.at[l, q], w_send.at[l, dq], w_recv.at[l, dq], dq, shift[l])
-            b.start()
-            a.start()
-            waits.extend([a.wait_send, b.wait_send])
-            pending += [(a.wait_recv, b.wait_recv)]
-        return pending
-
-    pending_w = [None] * layers
-    pending_w[0] = send_weights(0)
-
-    inputs = []
+    if pairs:
+        x_me = lax.axis_index("img")
+        half = x_me % 2
+        twin = x_me + 1 - 2 * half
+        share_rows = KB * IB // 2
+        w_rows = pl.ds(pl.multiple_of(half * share_rows, share_rows), share_rows)
+        pl.semaphore_signal(
+            barrier, inc=1, device_id={"img": twin}, device_id_type=pl.DeviceIdType.MESH
+        )
+    else:
+        w_rows = pl.ds(0, KB * IB)
+
     for d, a, b in loads:
         a.wait()
         b.wait()
         masked = (val[d].astype(jnp.float32) * mask[d].astype(jnp.float32))
         if d:
             y0[d] = masked.astype(jnp.bfloat16)
-            x = remote(y0.at[d], xin.at[d], in_send.at[d], in_recv.at[d], d, 0)
+        else:
+            ya[pl.ds(q * run_blocks, run_blocks)] = masked.reshape(run_blocks, IB, lanes)
+    for a in own:
+        a.wait()
+    pl.semaphore_wait(barrier, len(partners) + (1 if pairs else 0))
+
+    waits = []
+    index_waits = [[] for _ in range(layers)]
+    weight_sends = []
+    weight_waits = [[] for _ in range(layers)]
+    for l in range(layers):
+        for dq in order + [0]:
+            if dq == 0 and shift[l] % classes == 0:
+                a = pltpu.make_async_copy(w_src.at[l], wt.at[l, q], w_recv.at[l, 0])
+                b = pltpu.make_async_copy(i_src.at[l], idx_v.at[l, q], i_recv.at[l, 0])
+                a.start()
+                b.start()
+                weight_waits[l].append(a.wait)
+                index_waits[l].append(b.wait)
+                continue
+            b = remote(i_src.at[l], idx_v.at[l, q], i_send.at[l, dq], i_recv.at[l, dq], dq, shift[l])
+            a = remote(
+                w_src.at[l, w_rows], wt.at[l, q, w_rows], w_send.at[l, dq], w_recv.at[l, dq], dq, shift[l]
+            )
+            b.start()
+            a.start()
+            waits.extend([a.wait_send, b.wait_send])
+            index_waits[l].append(b.wait_recv)
+            weight_sends.append((l, dq, a))
+
+    inputs = []
+    for d in order:
+        x = remote(y0.at[d], xin.at[d], in_send.at[d], in_recv.at[d], d, 0)
+        x.start()
+        waits.append(x.wait_send)
+        inputs.append((d, x))
+
+    for l, dq, a in weight_sends:
+        a.wait_recv()
+        if pairs:
+            here = wt.at[l, (q + group - dq) % group, w_rows]
+            x = pltpu.make_async_remote_copy(
+                src_ref=here, dst_ref=here, send_sem=f_send.at[l, dq], recv_sem=f_recv.at[l, dq],
+                device_id={"img": twin}, device_id_type=pl.DeviceIdType.MESH,
+            )
             x.start()
             waits.append(x.wait_send)
-            inputs.append((d, x))
-        else:
-            ya[pl.ds(q * run_blocks, run_blocks)] = masked.reshape(run_blocks, IB, lanes)
-    for l in range(1, layers):
-        pending_w[l] = send_weights(l)
+            weight_waits[l].append(x.wait_recv)
+
+    index_copies = []
+    for l in range(layers):
+        for w in index_waits[l]:
+            w()
+        x = pltpu.make_async_copy(idx_v.at[l], idx_s.at[l], s_sem.at[l])
+        x.start()
+        index_copies.append(x)
 
     per = min(4, blocks)
     width = per * OB
@@ -117,18 +158,13 @@
     n_of = lax.broadcasted_iota(jnp.int32, (width, width), 1) // OB
 
     def prepare(l):
-        for a, b in pending_w[l]:
-            b()
-        c0 = pltpu.make_async_copy(idx_v.at[l], idx_s.at[l], s_sem.at[l])
-        c0.start()
-        for a, b in pending_w[l]:
-            a()
+        for w in weight_waits[l]:
+            w()
         for t in range(group):
             for g in range(blocks // per):
                 w = wt[l, t, :, g * width:(g + 1) * width].astype(jnp.float32)
                 wide = jnp.where(m_of == n_of, jnp.concatenate([w] * per, axis=0), 0.0)
                 wd[l, t, g] = wide.T.astype(jnp.bfloat16)
-        c0.wait()
 
     def advance(l, src, t):
         out = []
@@ -144,7 +180,10 @@
             out.append(clamped.astype(jnp.bfloat16))
         return out
 
-    prepare(0)
+    for l in range(layers):
+        prepare(l)
+    for x in index_copies:
+        x.wait()
     for d, x in inputs:
         x.wait_recv()
         s = (q + group - d) % group
@@ -156,7 +195,6 @@
             for g, y in enumerate(advance(l, src, t)):
                 first = t * run_blocks + g * width // IB
                 dst[first:first + width // IB] = y.astype(jnp.float32).reshape(width // IB, IB, lanes)
-        prepare(l + 1)
         src, dst = dst, src
 
     total = jnp.zeros((8, lanes), jnp.float32)
@@ -197,7 +235,7 @@
         w()
 
 
-def on_device(classes, image_values, image_mask, weights, block_index):
+def on_device(classes, pairs, image_values, image_mask, weights, block_index):
     layers, rows = weights.shape[:2]
     blocks = block_index.shape[1]
     columns = image_values.shape[1]
@@ -210,8 +248,9 @@
     V, S = pltpu.VMEM, pltpu.SMEM
     dma = pltpu.SemaphoreType.DMA
     any_spec = pl.BlockSpec(memory_space=pl.ANY)
+    operands = [pltpu.with_memory_space_constraint(v, pltpu.HBM) for v in (image_values, image_mask, wt, idx)]
     out, sums = pl.pallas_call(
-        functools.partial(kernel, (classes, layers, rows, blocks, lanes)),
+        functools.partial(kernel, (classes, pairs, layers, rows, blocks, lanes)),
         out_shape=(
             jax.ShapeDtypeStruct((rows, columns), bf16),
             jax.ShapeDtypeStruct((1, lanes // classes), f32),
@@ -221,6 +260,8 @@
         scratch_shapes=[
             V((group, rows, lanes), bf16),
             V((group, rows, lanes), i32),
+            V((layers, KB * IB, rows), bf16),
+            V((layers, KB, blocks), i32),
             V((group, rows, lanes), bf16),
             V((group, rows, lanes), bf16),
             V((group * rows // IB, IB, lanes), f32),
@@ -232,7 +273,8 @@
             V((group, rows, lanes), bf16),
             V((8, lanes), f32),
             V((classes, 8, lanes), f32),
-            dma((2, group)),
+            dma((2, group)), dma((2,)),
+            dma((layers, group)), dma((layers, group)),
             dma((group,)), dma((group,)),
             dma((layers, group)), dma((layers, group)),
             dma((layers, group)), dma((layers, group)),
@@ -240,8 +282,8 @@
             dma((group,)), dma((group,)),
             dma((classes,)), dma((classes,)),
         ],
-        compiler_params=pltpu.CompilerParams(collective_id=0, has_side_effects=True),
-    )(image_values, image_mask, wt, idx)
+        compiler_params=pltpu.CompilerParams(collective_id=0, has_side_effects=True, vmem_limit_bytes=16 * 1024 * 1024),
+    )(*operands)
     return out, sums.reshape(-1)
 
 
@@ -250,6 +292,6 @@
     in_specs = (P("neu", "img"), P("neu", "img"), P(None, "neu", None, None), P(None, "neu", None))
     out_specs = (P("neu", "img"), P(("img", "neu")))
     return jax.shard_map(
-        functools.partial(on_device, classes), mesh=mesh, in_specs=in_specs,
+        functools.partial(on_device, classes, mesh.shape["img"] % 2 == 0), mesh=mesh, in_specs=in_specs,
         out_specs=out_specs, check_vma=False,
     )

time: 30 us -> 26.2 us (0.87)
  the two profiles are of different devices: /device:TPU:1 before, /device:TPU:0 now
where the time goes in v2:
time: 26.2 us; the launch traced here: 26 us
  Pallas kernels  24.2 us (92%)
  local copies, waits for them, and re-layouts  1.22 us (5%)
  between operations  0.64 us (2%)
    pallas_call x1, Pallas kernels, on_device(): pl.pallas_call(functools.partial(kernel, (classes, pairs, layers, rows, b...  24.2 us
    unnamed x2, local copies, waits for them, and re-layouts  1.22 us

profile of v2, /device:TPU:0, one launch (start us, length us, event | category | flops | bytes accessed | tf_op | source)
XLA Modules:
  0.0 26.0 jit_solution(13096239838397833981)
XLA Ops:
  0.6 24.2 %shard_map.59 = (bf16[256,512]{1,0:T(8,128)(2,1)S(1)}, f32[1,32]{1,0:T(1,128)S(1)}) custom-call(bf16[256,512]{1,0:T(8,128)(2,1)} %val_hbm.1, s32[256,512]{1,0:T(8,128)} %mask_hbm.1, bf16[3,32,256]{2,1,0:T(8,128)(2,1)} %bitcast.6, s32[3,4,8]{2,1,0:T(4,128)} %bitcast.7), custom_call_target="tpu_custom_call" | custom-call | tf_op jit(solution)/shard_map/pallas_call | solution.py:252
  24.8 0.7 %copy.8 = bf16[256,512]{1,0:T(8,128)(2,1)} copy(bf16[256,512]{1,0:T(8,128)(2,1)S(1)} %get-tuple-element.8) | data formatting | bytes 524288
  25.5 0.5 %copy.9 = f32[32]{0:T(128)} copy(f32[32]{0:T(128)S(1)} %bitcast.5) | data formatting | bytes 256

commit v3 on v2

--- a/solution.py
+++ b/solution.py
@@ -45,7 +45,10 @@
             device_id={"neu": device(dq, dc)}, device_id_type=pl.DeviceIdType.MESH,
         )
 
-    order = [d for d in (2, 1, 3)]
+    order = [1, 3, 2]
+    order_w = [1, 3, 2]
+    order_in = [1, 2, 3]
+    order_out = [1, 3, 2]
 
     own = [
         pltpu.make_async_copy(wt_hbm, w_src, own_sem.at[0]),
@@ -106,7 +109,7 @@
     weight_sends = []
     weight_waits = [[] for _ in range(layers)]
     for l in range(layers):
-        for dq in order + [0]:
+        for dq in order_w + [0]:
             if dq == 0 and shift[l] % classes == 0:
                 a = pltpu.make_async_copy(w_src.at[l], wt.at[l, q], w_recv.at[l, 0])
                 b = pltpu.make_async_copy(i_src.at[l], idx_v.at[l, q], i_recv.at[l, 0])
@@ -126,7 +129,7 @@
             weight_sends.append((l, dq, a))
 
     inputs = []
-    for d in order:
+    for d in order_in:
         x = remote(y0.at[d], xin.at[d], in_send.at[d], in_recv.at[d], d, 0)
         x.start()
         waits.append(x.wait_send)
@@ -200,7 +203,7 @@
     total = jnp.zeros((8, lanes), jnp.float32)
     last = layers - 1
     outputs = []
-    for d in order + [0]:
+    for d in order_out + [0]:
         t = (q + d) % group
         for g, y in enumerate(advance(last, src, t)):
             tiles[d, g * width:(g + 1) * width, :] = y

time: 26.2 us -> 24.9 us (0.950)
  Pallas kernels: 24.2 us -> 22.8 us
    pallas_call x1, Pallas kernels: 24.2 us -> 22.8 us  [on_device(): pl.pallas_call(functools.partial(kernel, (classes, pairs, layers, rows, b...]
where the time goes in v3:
time: 24.9 us; the launch traced here: 24.6 us
  Pallas kernels  22.8 us (92%)
  local copies, waits for them, and re-layouts  1.22 us (5%)
  between operations  0.64 us (3%)
    pallas_call x1, Pallas kernels, on_device(): pl.pallas_call(functools.partial(kernel, (classes, pairs, layers, rows, b...  22.8 us
    unnamed x2, local copies, waits for them, and re-layouts  1.22 us

profile of v3, /device:TPU:0, one launch (start us, length us, event | category | flops | bytes accessed | tf_op | source)
XLA Modules:
  0.0 24.6 jit_solution(14544074356083312127)
XLA Ops:
  0.6 22.8 %shard_map.59 = (bf16[256,512]{1,0:T(8,128)(2,1)S(1)}, f32[1,32]{1,0:T(1,128)S(1)}) custom-call(bf16[256,512]{1,0:T(8,128)(2,1)} %val_hbm.1, s32[256,512]{1,0:T(8,128)} %mask_hbm.1, bf16[3,32,256]{2,1,0:T(8,128)(2,1)} %bitcast.6, s32[3,4,8]{2,1,0:T(4,128)} %bitcast.7), custom_call_target="tpu_custom_call" | custom-call | tf_op jit(solution)/shard_map/pallas_call | solution.py:255
  23.4 0.7 %copy.8 = bf16[256,512]{1,0:T(8,128)(2,1)} copy(bf16[256,512]{1,0:T(8,128)(2,1)S(1)} %get-tuple-element.8) | data formatting | bytes 524288
  24.1 0.5 %copy.9 = f32[32]{0:T(128)} copy(f32[32]{0:T(128)S(1)} %bitcast.5) | data formatting | bytes 256
